TPU v7x, 32 devices: a whole 2x2x4 slice. The times are simulated.
32 devices in a mesh: segment: 4 (over y, x), amp: 8 (over z, core).
Axes of the slice: x: 2, y: 2, z: 4, core: 2. Of those that a mesh axis runs over, the one named last changes fastest.
Arguments:
- states: float32 [4, 2097152], P('segment', 'amp'), may hold values from -6 to 6
- gate_blocks: float32 [4, 3, 128, 128], P('segment'), may hold values from -1 to 1, as said below
- kraus_picks: int32 [4, 4, 3, 7], P('segment'), may hold values from 0 to 3
- block_targets: int32 [4, 3], replicated, may hold values from 0 to 1
Outputs:
- final_states: float32 [4, 2097152], P('segment', 'amp')
- log_weights: float32 [4, 4], P('segment')
Inputs may be any that keep to these rules, and one draw needn't show every extreme that they name: Every block of gate_blocks is an orthogonal matrix, up to rounding.
All inputs are finite; a program needn't handle non-finite values.
Results may differ from a plain program's by a relative error of at most 0.0003.
Values sent between devices are 32-bit elements; how exact they have to be, the bound alone decides.
A program may use at most 64 MiB of HBM per device.

v0:
```python
import functools

import jax
import jax.numpy as jnp
from jax import lax
from jax.experimental import pallas as pl
from jax.experimental.pallas import tpu as pltpu
from jax.sharding import PartitionSpec as P

KEEP_FACTORS = (1.0, 0.9, 1.0, 0.97)
FLIP_FACTORS = (0.9, 1.0, 0.97, 1.0)
MESH = pl.DeviceIdType.MESH


def broadcast(block, axis, owner):
    block = jnp.where(lax.axis_index(axis) == owner, block, jnp.zeros_like(block))
    return lax.psum(block, axis)


def noise_factors(kraus_rows):
    qubit_count = kraus_rows.shape[-1]
    register = 2**qubit_count
    positions = jnp.arange(register, dtype=jnp.int32)
    product = jnp.ones(kraus_rows.shape[:-1] + (register,), jnp.float32)
    for qubit_pos in range(qubit_count):
        bit_value = jnp.right_shift(positions, qubit_count - 1 - qubit_pos) & 1
        column = kraus_rows[..., qubit_pos : qubit_pos + 1]
        low_value = jnp.zeros(column.shape, jnp.float32)
        high_value = jnp.zeros(column.shape, jnp.float32)
        for option in range(4):
            picked = (column == option).astype(jnp.float32)
            low_value = low_value + picked * KEEP_FACTORS[option]
            high_value = high_value + picked * FLIP_FACTORS[option]
        product = product * jnp.where(bit_value == 1, high_value, low_value)
    return product


def apply_gate(amplitudes, matrix, factors, target):

    def on_low(values):
        mixed_rows = jnp.einsum("bhmk,ik->bhmi", values, matrix, precision=lax.Precision.HIGHEST)
        return mixed_rows * factors[:, None, None, :]

    def on_high(values):
        mixed_rows = jnp.einsum("bjmk,ij->bimk", values, matrix, precision=lax.Precision.HIGHEST)
        return mixed_rows * factors[:, :, None, None]

    return lax.cond(target == 0, on_low, on_high, amplitudes)


def square_sums(values):
    return (values, jnp.sum(values * values, axis=(1, 2, 3)))


def body(states, gate_blocks, kraus_picks, block_targets):
    traj_here = states.shape[0]
    amp_local = states.shape[1]
    register = gate_blocks.shape[-1]
    blocks = gate_blocks.shape[1]
    middle = amp_local // (register * register)
    total_amps = amp_local * lax.axis_size("amp")
    sections = lax.axis_size("segment")
    amplitudes = states.reshape(traj_here, register, middle, register)
    first_local = jnp.sum(amplitudes * amplitudes, axis=(1, 2, 3))
    local_sums = [first_local]
    for section in range(sections):
        section_gates = broadcast(gate_blocks, "segment", section)[0]
        for block_pos in range(blocks):
            factors = noise_factors(kraus_picks[:, section, block_pos, :])
            amplitudes = apply_gate(
                amplitudes, section_gates[block_pos], factors, block_targets[section, block_pos]
            )
        amplitudes, local_sq = square_sums(
            lax.all_to_all(amplitudes, "amp", split_axis=1, concat_axis=1, tiled=True)
        )
        local_sums.append(local_sq)
    totals = lax.psum(jnp.stack(local_sums, axis=1), "amp")
    log_weights = jnp.log(totals[:, 1:] / totals[:, :-1])
    amplitudes = amplitudes / jnp.sqrt(totals[:, -1] / total_amps)[:, None, None, None]
    return (amplitudes.reshape(traj_here, amp_local), log_weights)


def partner(index, k):
    result = index
    bit = 1
    while bit <= k:
        if k & bit:
            result = result + bit * (1 - 2 * ((index // bit) % 2))
        bit *= 2
    return result


def split(values):
    high = values.astype(jnp.bfloat16)
    low = (values - high.astype(jnp.float32)).astype(jnp.bfloat16)
    return high, low


def left_form(matrix):
    return jnp.concatenate(split(matrix), axis=1)


def right_form(matrix):
    row = jnp.concatenate(split(matrix), axis=1)
    return jnp.concatenate([row, row], axis=0)


def multiply(left, right):
    both = jnp.dot(left, right, preferred_element_type=jnp.float32)
    half = both.shape[1] // 2
    return both[:, :half] + both[:, half:]


def fold_rows(values):
    squares = values * values
    return jnp.sum(squares.reshape(-1, 8, squares.shape[-1]), axis=0)


def row_factors(picks_ref, row, qubits, shape):
    positions = lax.broadcasted_iota(jnp.int32, shape, 0)
    product = jnp.ones(shape, jnp.float32)
    for q in range(qubits):
        pick = picks_ref[row * qubits + q]
        keep = jnp.float32(KEEP_FACTORS[0])
        flip = jnp.float32(FLIP_FACTORS[0])
        for option in range(1, 4):
            keep = jnp.where(pick == option, jnp.float32(KEEP_FACTORS[option]), keep)
            flip = jnp.where(pick == option, jnp.float32(FLIP_FACTORS[option]), flip)
        bit = jnp.right_shift(positions, qubits - 1 - q) & 1
        product = product * jnp.where(bit == 1, flip, keep)
    return product


def circuit_kernel(
    peers, sections, blocks, qubits, chunks, total_amps,
    x_hbm, gates_hbm, picks_ref, targets_ref,
    out_ref, logs_ref,
    xs, yin, ov, gates, low_form, high_form, partial, sums,
    x_sem, own_sem, gate_sem, gsend, grecv, isend, irecv, osend, orecv, ssend, srecv,
):
    seg = lax.axis_index("segment")
    amp = lax.axis_index("amp")
    reg = gates.shape[-1]
    middle = chunks * peers
    order = list(range(peers - 1, 0, -1))

    loads = []
    for chunk in range(chunks):
        for d in range(peers):
            m = chunk * peers + d
            load = pltpu.make_async_copy(x_hbm.at[:, m, 0], xs.at[m], x_sem.at[m])
            load.start()
            loads.append(load)
    gate_load = pltpu.make_async_copy(gates_hbm, gates.at[seg], gate_sem)
    gate_load.start()
    own_loads = []
    for chunk in range(chunks):
        own = pltpu.make_async_copy(
            x_hbm.at[:, chunk * peers + amp, 0], yin.at[chunk, amp], own_sem.at[chunk]
        )
        own.start()
        own_loads.append(own)

    barrier = pltpu.get_barrier_semaphore()
    for k in order:
        pl.semaphore_signal(
            barrier, inc=1, device_id={"amp": partner(amp, k)}, device_id_type=MESH
        )
    for k in range(1, sections):
        pl.semaphore_signal(
            barrier, inc=1, device_id={"segment": partner(seg, k)}, device_id_type=MESH
        )
    pl.semaphore_wait(barrier, peers - 1 + sections - 1)

    for load in loads:
        load.wait()

    in_copies = []
    for chunk in range(chunks):
        copies = []
        for k in order:
            peer = partner(amp, k)
            copy = pltpu.make_async_remote_copy(
                src_ref=xs.at[chunk * peers + peer],
                dst_ref=yin.at[chunk, amp],
                send_sem=isend.at[chunk, k],
                recv_sem=irecv.at[chunk, k],
                device_id={"amp": peer},
                device_id_type=MESH,
            )
            copy.start()
            copies.append(copy)
        in_copies.append(copies)

    gate_load.wait()
    gate_copies = []
    for k in range(1, sections):
        copy = pltpu.make_async_remote_copy(
            src_ref=gates.at[seg],
            dst_ref=gates.at[seg],
            send_sem=gsend.at[k],
            recv_sem=grecv.at[k],
            device_id={"segment": partner(seg, k)},
            device_id_type=MESH,
        )
        copy.start()
        gate_copies.append(copy)
    for copy in gate_copies:
        copy.wait_recv()

    rows_at = lax.broadcasted_iota(jnp.int32, (reg, reg), 0)
    columns_at = lax.broadcasted_iota(jnp.int32, (reg, reg), 1)
    identity = jnp.where(rows_at == columns_at, jnp.float32(1.0), jnp.float32(0.0))

    def build(section, carry):
        low = high = None
        for b in range(blocks):
            row = section * blocks + b
            damped = gates[section, b] * row_factors(picks_ref, row, qubits, (reg, reg))
            is_low = targets_ref[row] == 0
            for_low = jnp.where(is_low, damped, identity)
            for_high = jnp.where(is_low, identity, damped)
            if b == 0:
                low, high = for_low, for_high
            else:
                low = multiply(left_form(for_low), right_form(low))
                high = multiply(left_form(for_high), right_form(high))
        low_form[section] = right_form(low.T)
        high_form[section] = left_form(high)
        return carry

    lax.fori_loop(0, sections, build, 0)

    inner = reg // peers
    partial[...] = jnp.zeros_like(partial)

    def apply_section(chunk, section, swapped):
        low = low_form[section]
        high = high_form[section]
        total = jnp.zeros((8, reg), jnp.float32)
        for slab in range(peers):
            if swapped:
                value = yin[chunk, :, slab * inner : (slab + 1) * inner, :].reshape(reg, reg)
            else:
                value = yin[chunk, slab]
            value = multiply(left_form(value), low)
            value = multiply(high, right_form(value))
            total = total + fold_rows(value)
            if swapped:
                yin[chunk, :, slab * inner : (slab + 1) * inner, :] = value.reshape(
                    peers, inner, reg
                )
            else:
                yin[chunk, slab] = value
        partial[section + 1] = partial[section + 1] + total

    out_copies = []
    for chunk in range(chunks):
        own_loads[chunk].wait()
        for copy in in_copies[chunk]:
            copy.wait_recv()
        first = jnp.zeros((8, reg), jnp.float32)
        for slab in range(peers):
            first = first + fold_rows(yin[chunk, slab])
        partial[0] = partial[0] + first

        def pair(i, carry, chunk=chunk):
            apply_section(chunk, 2 * i, False)
            apply_section(chunk, 2 * i + 1, True)
            return carry

        lax.fori_loop(0, sections // 2, pair, 0)

        if chunk == chunks - 1:
            for s in range(sections + 1):
                sums[amp, s : s + 1, :] = jnp.sum(partial[s], axis=0, keepdims=True)
            sum_copies = []
            for k in order:
                copy = pltpu.make_async_remote_copy(
                    src_ref=sums.at[amp],
                    dst_ref=sums.at[amp],
                    send_sem=ssend.at[k],
                    recv_sem=srecv.at[k],
                    device_id={"amp": partner(amp, k)},
                    device_id_type=MESH,
                )
                copy.start()
                sum_copies.append(copy)
        copies = []
        for k in order:
            peer = partner(amp, k)
            copy = pltpu.make_async_remote_copy(
                src_ref=yin.at[chunk, peer],
                dst_ref=ov.at[chunk, amp],
                send_sem=osend.at[chunk, k],
                recv_sem=orecv.at[chunk, k],
                device_id={"amp": peer},
                device_id_type=MESH,
            )
            copy.start()
            copies.append(copy)
        out_copies.append(copies)

    for copy in sum_copies:
        copy.wait_recv()
    totals = []
    for s in range(sections + 1):
        total = sums[0, s : s + 1, :]
        for d in range(1, peers):
            total = total + sums[d, s : s + 1, :]
        totals.append(jnp.sum(total, axis=1, keepdims=True))
    lanes = lax.broadcasted_iota(jnp.int32, (1, reg), 1)
    logs = jnp.zeros((1, reg), jnp.float32)
    for s in range(sections):
        logs = jnp.where(lanes == s, jnp.log(totals[s + 1] / totals[s]), logs)
    logs_ref[...] = logs[:, :sections]
    scale = 1.0 / jnp.sqrt(totals[sections] / total_amps)
    scale = jnp.broadcast_to(scale, (1, reg))

    for chunk in range(chunks):
        m = chunk * peers + amp
        out_ref[pl.ds(m, reg, stride=middle), :] = yin[chunk, amp] * scale
    for chunk in range(chunks):
        for at, k in reversed(list(enumerate(order))):
            out_copies[chunk][at].wait_recv()
            m = chunk * peers + partner(amp, k)
            out_ref[pl.ds(m, reg, stride=middle), :] = ov[chunk, partner(amp, k)] * scale

    for copies in in_copies + out_copies + [gate_copies, sum_copies]:
        for copy in copies:
            copy.wait_send()


def step(states, gate_blocks, kraus_picks, block_targets):
    traj_here, amp_local = states.shape
    reg = gate_blocks.shape[-1]
    blocks = gate_blocks.shape[1]
    qubits = kraus_picks.shape[-1]
    peers = lax.axis_size("amp")
    sections = lax.axis_size("segment")
    middle = amp_local // (reg * reg)
    fits = (
        traj_here == 1
        and gate_blocks.shape[0] == 1
        and middle % peers == 0
        and peers & (peers - 1) == 0
        and sections & (sections - 1) == 0
        and sections % 2 == 0
        and sections < 8
        and reg == 128
        and reg % (8 * peers) == 0
    )
    if not fits:
        return body(states, gate_blocks, kraus_picks, block_targets)
    chunks = middle // peers
    kernel = functools.partial(
        circuit_kernel, peers, sections, blocks, qubits, chunks, amp_local * peers
    )
    f32 = jnp.float32
    dma = pltpu.SemaphoreType.DMA
    out, logs = pl.pallas_call(
        kernel,
        out_shape=(
            jax.ShapeDtypeStruct((reg * middle, reg), f32),
            jax.ShapeDtypeStruct((1, sections), f32),
        ),
        in_specs=[
            pl.BlockSpec(memory_space=pl.ANY),
            pl.BlockSpec(memory_space=pl.ANY),
            pl.BlockSpec(memory_space=pltpu.SMEM),
            pl.BlockSpec(memory_space=pltpu.SMEM),
        ],
        out_specs=(
            pl.BlockSpec(memory_space=pltpu.VMEM),
            pl.BlockSpec(memory_space=pltpu.VMEM),
        ),
        scratch_shapes=[
            pltpu.VMEM((middle, reg, reg), f32),
            pltpu.VMEM((chunks, peers, reg, reg), f32),
            pltpu.VMEM((chunks, peers, reg, reg), f32),
            pltpu.VMEM((sections, blocks, reg, reg), f32),
            pltpu.VMEM((sections, 2 * reg, 2 * reg), jnp.bfloat16),
            pltpu.VMEM((sections, reg, 2 * reg), jnp.bfloat16),
            pltpu.VMEM((sections + 1, 8, reg), f32),
            pltpu.VMEM((peers, 8, reg), f32),
            dma((middle,)),
            dma((chunks,)),
            dma,
            dma((sections,)),
            dma((sections,)),
            dma((chunks, peers)),
            dma((chunks, peers)),
            dma((chunks, peers)),
            dma((chunks, peers)),
            dma((peers,)),
            dma((peers,)),
        ],
        compiler_params=pltpu.CompilerParams(collective_id=0, has_side_effects=True),
    )(
        states.reshape(reg, middle, 1, reg),
        gate_blocks[0],
        kraus_picks.reshape(-1),
        block_targets.reshape(-1),
    )
    return out.reshape(1, amp_local), logs


def solution(mesh):
    in_specs = (
        P("segment", "amp"),
        P("segment", None, None, None),
        P("segment", None, None, None),
        P(),
    )
    out_specs = (P("segment", "amp"), P("segment", None))
    return jax.shard_map(step, mesh=mesh, in_specs=in_specs, out_specs=out_specs, check_vma=False)
```

profile of v0, /device:TPU:0, one launch (start us, length us, event | category | flops | bytes accessed | tf_op | source)
XLA Modules:
  0.0 60.6 jit_solution(6615252284659015620)
XLA Ops:
  0.6 0.0 copy-start
  0.6 1.3 %reshape.18.targets_ref = s32[12]{0:T(128)} reshape(s32[4,3]{1,0:T(4,128)} %param.7) | data formatting | bytes 96 | tf_op jit(solution)/shard_map/reshape | solution.py:403
  1.9 0.0 copy-done
  1.9 0.6 reshape.17.picks_ref
  2.5 55.5 %shard_map.59 = (f32[2048,128]{1,0:T(8,128)}, f32[1,4]{1,0:T(1,128)}) custom-call(f32[128,16,1,128]{3,2,1,0:T(1,128)} %bitcast.3, f32[3,128,128]{2,1,0:T(8,128)} %bitcast.5, s32[84]{0:T(128)} %reshape.17.picks_ref, s32[12]{0:T(128)} %reshape.18.targets_ref), custom_call_target="tpu_custom_call" | custom-call | tf_op jit(solution)/shard_map/pallas_call | solution.py:361
  58.1 0.0 copy-start.1
  58.1 2.0 %copy.10 = f32[1,262144]{1,0:T(1,128)} copy(f32[1,262144]{1,0:T(1,128)} %bitcast.4) | data formatting | bytes 2097152
  60.1 0.0 copy-done.1
  60.1 0.5 copy.11
  (1 shorter events, 0.0 us)
Async XLA Ops:
  0.6 1.3 %copy-start = (s32[1,4,3,7]{3,1,2,0:T(4,128)S(1)}, s32[1,4,3,7]{3,1,2,0:T(4,128)}, u32[]{:S(2)}) copy-start(s32[1,4,3,7]{3,1,2,0:T(4,128)} %param.6) | copy-start | bytes 1012
  58.1 2.1 %copy-start.1 = (f32[1,4]{1,0:T(1,128)S(1)}, f32[1,4]{1,0:T(1,128)}, u32[]{:S(2)}) copy-start(f32[1,4]{1,0:T(1,128)} %get-tuple-element.9) | copy-start | bytes 52
where the time goes:
time: 60.8 us; the launch traced here: 60.6 us
  Pallas kernels  55.5 us (91%)
  local copies, waits for them, and re-layouts  4.45 us (7%)
  between operations  0.66 us (1%)
    pallas_call x1, Pallas kernels, step(): pl.pallas_call(kernel, out_shape=(jax.ShapeDtypeStruct((reg * middle, reg...  55.5 us
    unnamed x7, local copies, waits for them, and re-layouts  2.57 us
    reshape x1, local copies, waits for them, and re-layouts, step(): block_targets.reshape(-1)  1.28 us

commit v1 on v0

--- a/solution.py
+++ b/solution.py
@@ -116,11 +116,11 @@
     return jnp.sum(squares.reshape(-1, 8, squares.shape[-1]), axis=0)
 
 
-def row_factors(picks_ref, row, qubits, shape):
+def row_factors(picks_ref, section, block, qubits, shape):
     positions = lax.broadcasted_iota(jnp.int32, shape, 0)
     product = jnp.ones(shape, jnp.float32)
     for q in range(qubits):
-        pick = picks_ref[row * qubits + q]
+        pick = picks_ref[0, block, section, q]
         keep = jnp.float32(KEEP_FACTORS[0])
         flip = jnp.float32(FLIP_FACTORS[0])
         for option in range(1, 4):
@@ -215,9 +215,9 @@
     def build(section, carry):
         low = high = None
         for b in range(blocks):
-            row = section * blocks + b
-            damped = gates[section, b] * row_factors(picks_ref, row, qubits, (reg, reg))
-            is_low = targets_ref[row] == 0
+            factors = row_factors(picks_ref, section, b, qubits, (reg, reg))
+            damped = gates[section, b] * factors
+            is_low = targets_ref[section, b] == 0
             for_low = jnp.where(is_low, damped, identity)
             for_high = jnp.where(is_low, identity, damped)
             if b == 0:
@@ -361,8 +361,8 @@
     out, logs = pl.pallas_call(
         kernel,
         out_shape=(
-            jax.ShapeDtypeStruct((reg * middle, reg), f32),
-            jax.ShapeDtypeStruct((1, sections), f32),
+            pltpu.VMEM((reg * middle, reg), f32),
+            pltpu.VMEM((1, sections), f32),
         ),
         in_specs=[
             pl.BlockSpec(memory_space=pl.ANY),
@@ -399,8 +399,8 @@
     )(
         states.reshape(reg, middle, 1, reg),
         gate_blocks[0],
-        kraus_picks.reshape(-1),
-        block_targets.reshape(-1),
+        jnp.swapaxes(kraus_picks, 1, 2),
+        block_targets,
     )
     return out.reshape(1, amp_local), logs
 

time: 60.8 us -> 57 us (0.938)
  local copies, waits for them, and re-layouts: 4.45 us -> 1.48 us
  Pallas kernels: 55.5 us -> 54.7 us
    reshape x2 -> x0, local copies, waits for them, and re-layouts: 1.88 us -> none  [the longest x1 1.28 us: step(): block_targets.reshape(-1)]
    unnamed x7 -> x2, local copies, waits for them, and re-layouts: 2.57 us -> 1.48 us
    pallas_call x1, Pallas kernels: 55.5 us -> 54.7 us  [step(): pl.pallas_call(kernel, out_shape=(pltpu.VMEM((reg * middle, reg), f32), p...]
where the time goes in v1:
time: 57 us; the launch traced here: 56.8 us
  Pallas kernels  54.7 us (96%)
  local copies, waits for them, and re-layouts  1.48 us (3%)
  between operations  0.64 us (1%)
    pallas_call x1, Pallas kernels, step(): pl.pallas_call(kernel, out_shape=(pltpu.VMEM((reg * middle, reg), f32), p...  54.7 us
    unnamed x2, local copies, waits for them, and re-layouts  1.48 us

profile of v1, /device:TPU:0, one launch (start us, length us, event | category | flops | bytes accessed | tf_op | source)
XLA Modules:
  0.0 56.8 jit_solution(4329027673315905932)
XLA Ops:
  0.6 54.7 %shard_map.59 = (f32[2048,128]{1,0:T(8,128)S(1)}, f32[1,4]{1,0:T(1,128)S(1)}) custom-call(f32[128,16,1,128]{3,2,1,0:T(1,128)} %bitcast.5, f32[3,128,128]{2,1,0:T(8,128)} %bitcast.6, s32[1,3,4,7]{3,2,1,0:T(4,128)} %bitcast.7, s32[4,3]{1,0:T(4,128)} %targets_ref.1), custom_call_target="tpu_custom_call" | custom-call | tf_op jit(solution)/shard_map/pallas_call | solution.py:361
  55.3 1.0 %copy.8 = f32[1,262144]{1,0:T(1,128)} copy(f32[1,262144]{1,0:T(1,128)S(1)} %bitcast.4) | data formatting | bytes 2097152
  56.3 0.5 copy.9

commit v2 on v1

--- a/solution.py
+++ b/solution.py
@@ -137,6 +137,7 @@
     out_ref, logs_ref,
     xs, yin, ov, gates, low_form, high_form, partial, sums,
     x_sem, own_sem, gate_sem, gsend, grecv, isend, irecv, osend, orecv, ssend, srecv,
+    entered,
 ):
     seg = lax.axis_index("segment")
     amp = lax.axis_index("amp")
@@ -161,26 +162,12 @@
         own.start()
         own_loads.append(own)
 
-    barrier = pltpu.get_barrier_semaphore()
-    for k in order:
-        pl.semaphore_signal(
-            barrier, inc=1, device_id={"amp": partner(amp, k)}, device_id_type=MESH
-        )
-    for k in range(1, sections):
-        pl.semaphore_signal(
-            barrier, inc=1, device_id={"segment": partner(seg, k)}, device_id_type=MESH
-        )
-    pl.semaphore_wait(barrier, peers - 1 + sections - 1)
-
-    for load in loads:
-        load.wait()
-
     in_copies = []
     for chunk in range(chunks):
-        copies = []
+        copies = {}
         for k in order:
             peer = partner(amp, k)
-            copy = pltpu.make_async_remote_copy(
+            copies[k] = pltpu.make_async_remote_copy(
                 src_ref=xs.at[chunk * peers + peer],
                 dst_ref=yin.at[chunk, amp],
                 send_sem=isend.at[chunk, k],
@@ -188,9 +175,72 @@
                 device_id={"amp": peer},
                 device_id_type=MESH,
             )
-            copy.start()
-            copies.append(copy)
         in_copies.append(copies)
+
+    def tell(semaphore, axis, index, k):
+        pl.semaphore_signal(
+            semaphore, inc=1, device_id={axis: partner(index, k)}, device_id_type=MESH
+        )
+
+    barrier = pltpu.get_barrier_semaphore()
+    if peers == 8 and sections == 4:
+        pair_at = amp // 2
+        inner_pair = (pair_at + 1) // 2 % 2
+        is_inner = inner_pair == 1
+        for k in (1, 2):
+            tell(barrier, "segment", seg, k)
+        for k in (1, 2, 3):
+            tell(barrier, "amp", amp, k)
+
+        @pl.when(is_inner)
+        def _():
+            tell(barrier, "amp", amp, 6)
+            tell(barrier, "amp", amp, 7)
+
+        for load in loads:
+            load.wait()
+        pl.semaphore_wait(barrier, 5 + 2 * inner_pair)
+
+        @pl.when(is_inner)
+        def _():
+            tell(entered.at[0], "amp", amp, 2)
+            tell(entered.at[0], "amp", amp, 6)
+            in_copies[0][6].start()
+            in_copies[0][7].start()
+
+        tell(entered.at[2], "segment", seg, 1)
+        pl.semaphore_wait(entered.at[0], 1)
+
+        @pl.when(is_inner)
+        def _():
+            tell(entered.at[1], "amp", amp, 2)
+
+        in_copies[0][4].start()
+        in_copies[0][5].start()
+
+        @pl.when(jnp.logical_not(is_inner))
+        def _():
+            pl.semaphore_wait(entered.at[1], 1)
+            in_copies[0][6].start()
+            in_copies[0][7].start()
+
+        for k in (3, 2, 1):
+            in_copies[0][k].start()
+        rest = in_copies[1:]
+        pl.semaphore_wait(entered.at[2], 1)
+    else:
+        for k in order:
+            tell(barrier, "amp", amp, k)
+        for k in range(1, sections):
+            tell(barrier, "segment", seg, k)
+        for load in loads:
+            load.wait()
+        pl.semaphore_wait(barrier, peers - 1 + sections - 1)
+        rest = in_copies
+    for copies in rest:
+        for k in order:
+            copies[k].start()
+    in_copies = [list(copies.values()) for copies in in_copies]
 
     gate_load.wait()
     gate_copies = []
@@ -255,6 +305,7 @@
         partial[section + 1] = partial[section + 1] + total
 
     out_copies = []
+    order_out = [5, 4, 7, 6, 3, 2, 1]
     for chunk in range(chunks):
         own_loads[chunk].wait()
         for copy in in_copies[chunk]:
@@ -287,7 +338,7 @@
                 copy.start()
                 sum_copies.append(copy)
         copies = []
-        for k in order:
+        for k in order_out:
             peer = partner(amp, k)
             copy = pltpu.make_async_remote_copy(
                 src_ref=yin.at[chunk, peer],
@@ -321,7 +372,7 @@
         m = chunk * peers + amp
         out_ref[pl.ds(m, reg, stride=middle), :] = yin[chunk, amp] * scale
     for chunk in range(chunks):
-        for at, k in reversed(list(enumerate(order))):
+        for at, k in reversed(list(enumerate(order_out))):
             out_copies[chunk][at].wait_recv()
             m = chunk * peers + partner(amp, k)
             out_ref[pl.ds(m, reg, stride=middle), :] = ov[chunk, partner(amp, k)] * scale
@@ -394,6 +445,7 @@
             dma((chunks, peers)),
             dma((peers,)),
             dma((peers,)),
+            pltpu.SemaphoreType.REGULAR((3,)),
         ],
         compiler_params=pltpu.CompilerParams(collective_id=0, has_side_effects=True),
     )(

time: 57 us -> 54.4 us (0.954)
  Pallas kernels: 54.7 us -> 52.1 us
    pallas_call x1, Pallas kernels: 54.7 us -> 52.1 us  [step(): pl.pallas_call(kernel, out_shape=(pltpu.VMEM((reg * middle, reg), f32), p...]
where the time goes in v2:
time: 54.4 us; the launch traced here: 54.2 us
  Pallas kernels  52.1 us (96%)
  local copies, waits for them, and re-layouts  1.48 us (3%)
  between operations  0.64 us (1%)
    pallas_call x1, Pallas kernels, step(): pl.pallas_call(kernel, out_shape=(pltpu.VMEM((reg * middle, reg), f32), p...  52.1 us
    unnamed x2, local copies, waits for them, and re-layouts  1.48 us

profile of v2, /device:TPU:0, one launch (start us, length us, event | category | flops | bytes accessed | tf_op | source)
XLA Modules:
  0.0 54.2 jit_solution(8490598166374869127)
XLA Ops:
  0.6 52.1 %shard_map.59 = (f32[2048,128]{1,0:T(8,128)S(1)}, f32[1,4]{1,0:T(1,128)S(1)}) custom-call(f32[128,16,1,128]{3,2,1,0:T(1,128)} %bitcast.5, f32[3,128,128]{2,1,0:T(8,128)} %bitcast.6, s32[1,3,4,7]{3,2,1,0:T(4,128)} %bitcast.7, s32[4,3]{1,0:T(4,128)} %targets_ref.1), custom_call_target="tpu_custom_call" | custom-call | tf_op jit(solution)/shard_map/pallas_call | solution.py:412
  52.7 1.0 %copy.8 = f32[1,262144]{1,0:T(1,128)} copy(f32[1,262144]{1,0:T(1,128)S(1)} %bitcast.4) | data formatting | bytes 2097152
  53.7 0.5 copy.9
